TPU v7x, 32 devices: a whole 2x2x4 slice. The times are simulated.
32 devices in a mesh: blk: 4 (over z), tp: 8 (over y, x, core).
Axes of the slice: x: 2, y: 2, z: 4, core: 2. Of those that a mesh axis runs over, the one named last changes fastest.
Arguments:
- input_pool: bfloat16 [4096, 1792], P(None, 'tp'), may hold values from -6 to 6
- teacher_pool: bfloat16 [4096, 1792], P(None, 'tp'), may hold values from -6 to 6
- gate_weight: bfloat16 [1792, 9472], P(None, 'tp'), may hold values from -0.125 to 0.125
- up_weight: bfloat16 [1792, 9472], P(None, 'tp'), may hold values from -0.125 to 0.125
- params: float32 [4, 9472, 1792], P('blk', 'tp'), may hold values from -6 to 6
- batch_ids: int32 [4, 1024], replicated, may hold values from 0 to 4095
- cycle_order: int32 [4], replicated, may hold values from 0 to 3, each once
- edge_weight: float32 [4], replicated, may hold values from 0.1 to 0.45
Outputs:
- updated: float32 [4, 9472, 1792], P('blk', 'tp')
Inputs may be any that keep to these rules, and one draw needn't show every extreme that they name: `cycle_order`: the 4 cycle positions name 4 different agents.
All inputs are finite; a program needn't handle non-finite values.
Results may differ from a plain program's by a relative error of at most 0.0061.
Values may be sent and summed in bfloat16 or wider, within the bound.
A program may use at most 128 MiB of HBM per device.

v0:
```python
import jax
import jax.numpy as jnp
from jax import lax
from jax.sharding import PartitionSpec as P


def shifted(array, axis, by):
    count = lax.axis_size(axis)
    return lax.ppermute(array, axis, [(i, (i + by) % count) for i in range(count)])


def body(
    input_pool, teacher_pool, gate_weight, up_weight, params, batch_ids, cycle_order, edge_weight
):
    step_rate = 2.0
    groups = lax.axis_size("tp")
    place = lax.axis_index("blk")
    agents = cycle_order.shape[0]
    slots = jnp.arange(agents, dtype=jnp.int32)
    here = slots == place
    before = slots == (place + agents - 1) % agents
    agent = jnp.sum(jnp.where(here, cycle_order, 0))
    weight_next = jnp.sum(jnp.where(here, edge_weight, 0.0))
    weight_prev = jnp.sum(jnp.where(before, edge_weight, 0.0))
    weight_self = 1.0 - weight_next - weight_prev
    batch = lax.dynamic_slice_in_dim(batch_ids, agent, 1, 0)[0]
    inputs_local = jnp.take(input_pool, batch, axis=0)
    teacher_local = jnp.take(teacher_pool, batch, axis=0)
    hidden_dev = gate_weight.shape[1]
    scale = float(hidden_dev * groups) ** (-0.5)
    rows = lax.all_gather(inputs_local, "tp", axis=1, tiled=True)
    gate = jnp.dot(rows, gate_weight, preferred_element_type=jnp.float32)
    up = jnp.dot(rows, up_weight, preferred_element_type=jnp.float32)
    teacher = lax.all_gather(teacher_local, "tp", axis=1, tiled=True)
    gate, up, teacher_full = (gate, up, teacher)
    hidden = (jax.nn.silu(gate) * up).astype(jnp.bfloat16)

    def gradient(weights):
        weights_half = weights.astype(jnp.bfloat16)
        partial_out = scale * jnp.dot(hidden, weights_half, preferred_element_type=jnp.float32)
        output = lax.psum(partial_out, "tp")
        resid = (output - teacher_full.astype(jnp.float32)).astype(jnp.bfloat16)
        return scale * lax.dot_general(
            hidden, resid, (((0,), (0,)), ((), ())), preferred_element_type=jnp.float32
        )

    start_field = params[0]
    grad_first = gradient(start_field)

    def mix_two(field):
        lower = shifted(field, "blk", 1)
        upper = shifted(field, "blk", -1)
        return weight_self * field + weight_next * upper + weight_prev * lower

    moved = mix_two(start_field) - step_rate * grad_first
    combined = moved - step_rate * grad_first
    grad_second = gradient(moved)
    result = mix_two(combined) - step_rate * (grad_second - grad_first)
    return result[None]


def solution(mesh):
    placed = (
        P(None, "tp"),
        P(None, "tp"),
        P(None, "tp"),
        P(None, "tp"),
        P("blk", "tp", None),
        P(),
        P(),
        P(),
    )
    return jax.shard_map(
        body, mesh=mesh, in_specs=placed, out_specs=P("blk", "tp", None), check_vma=False
    )
```

profile of v0, /device:TPU:0, one launch (start us, length us, event | category | flops | bytes accessed | tf_op | source)
XLA Modules:
  0.0 809.0 jit_solution(17603481513020024617)
XLA Ops:
  6.5 1.3 fusion.11
  9.8 4.0 copy.11
  13.8 3.2 copy.13
  17.0 5.3 gather_fusion
  22.4 3.9 gather_fusion.1
  26.5 1.0 copy.12
  28.6 5.1 collective-permute-start
  33.7 31.0 %all-gather.3.cloned.1.call-done = bf16[1024,1792]{0,1:T(8,128)(2,1)} async-done(((bf16[1024,224]{0,1:T(8,128)(2,1)}), bf16[1024,1792]{0,1:T(8,128)(2,1)}) %all-gather.3.cloned.1.call-update) | async-done | bytes 3670032 | tf_op jit(solution)/shard_map/all_gather | solution.py:31
  64.8 7.6 fusion.17
  72.4 8.0 multiply_convert_fusion
  80.4 1.5 copy-done.2
  81.8 7.2 convolution_multiply_fusion.2
  91.6 9.5 %all-gather.5.cloned.1.call-done = bf16[1024,1792]{0,1:T(8,128)(2,1)} async-done(((bf16[1024,224]{0,1:T(8,128)(2,1)}), bf16[1024,1792]{0,1:T(8,128)(2,1)}) %all-gather.5.cloned.1.call-update) | async-done | bytes 3670032 | tf_op jit(solution)/shard_map/all_gather | solution.py:34
  101.1 115.9 %collective-permute-done = f32[1184,1792]{1,0:T(8,128)} collective-permute-done((f32[1184,1792]{1,0:T(8,128)}, f32[1184,1792]{1,0:T(8,128)}, u32[]{:S(2)}, u32[]{:S(2)}) %collective-permute-start) | collective-permute-done | bytes 8486944 | tf_op jit(solution)/shard_map/ppermute | solution.py:9
  217.0 181.6 %collective-permute-done.1 = f32[1184,1792]{1,0:T(8,128)} collective-permute-done((f32[1184,1792]{1,0:T(8,128)}, f32[1184,1792]{1,0:T(8,128)}, u32[]{:S(2)}, u32[]{:S(2)}) %collective-permute-start.1) | collective-permute-done | bytes 8486944 | tf_op jit(solution)/shard_map/ppermute | solution.py:9
  398.6 22.6 %multiply_subtract_fusion = (f32[1184,1792]{1,0:T(8,128)}, bf16[1184,1792]{1,0:T(8,128)(2,1)S(1)}, f32[1184,1792]{1,0:T(8,128)}) fusion(f32[1184,1792]{1,0:T(8,128)} %collective-permute-done.1, f32[]{:T(128)} %get-tuple-element.7, f32[1184,1792]{1,0:T(8,128)} %collective-permute-done, f32[]{:T(128)} %get-tuple-element.6, f32[1,1184,1792]{2,1,0:T(8,128)} %param.14, ...), kind=kOutput, calls=%fused_computation.9 | convolution fusion | flops 4369899520 | bytes 60112908 | tf_op jit(solution)/shard_map/dot_general | solution.py:43
  421.2 1.6 collective-permute-start.3
  422.9 2.2 collective-permute-start.2
  425.1 8.7 %convolution_multiply_fusion.1 = f32[1024,1792]{0,1:T(8,128)} fusion(bf16[1024,1184]{0,1:T(8,128)(2,1)} %copy-done.2, bf16[1184,1792]{1,0:T(8,128)(2,1)S(1)} %get-tuple-element.9), kind=kOutput, calls=%fused_computation.13 | convolution fusion | flops 4347133952 | bytes 14008320 | tf_op jit(solution)/shard_map/dot_general | solution.py:40
  433.8 113.8 %all-reduce.5.cloned.1.call-done = f32[1024,1792]{0,1:T(8,128)} async-done(((f32[1024,1792]{0,1:T(8,128)}), f32[1024,1792]{0,1:T(8,128)}) %all-reduce.5.cloned.1.call-update) | async-done | bytes 7340048 | tf_op jit(solution)/shard_map/psum | solution.py:41
  547.6 12.8 %fusion.1 = f32[1184,1792]{1,0:T(8,128)} fusion(bf16[1024,1184]{0,1:T(8,128)(2,1)S(1)} %copy-done.3, f32[1184,1792]{1,0:T(8,128)} %get-tuple-element.12, f32[1024,1792]{0,1:T(8,128)} %all-reduce.5.cloned.1.call-done, bf16[1024,1792]{0,1:T(8,128)(2,1)} %all-gather.5.cloned.1.call-done), kind=kOutput, calls=%fused_computation.6 | convolution fusion | flops 4359290880 | bytes 30408704 | tf_op jit(solution)/shard_map/dot_general | solution.py:43
  560.5 48.3 %collective-permute-done.3 = f32[1184,1792]{1,0:T(8,128)} collective-permute-done((f32[1184,1792]{1,0:T(8,128)}, f32[1184,1792]{1,0:T(8,128)}, u32[]{:S(2)}, u32[]{:S(2)}) %collective-permute-start.3) | collective-permute-done | bytes 8486944 | tf_op jit(solution)/shard_map/ppermute | solution.py:9
  608.8 179.5 %collective-permute-done.2 = f32[1184,1792]{1,0:T(8,128)} collective-permute-done((f32[1184,1792]{1,0:T(8,128)}, f32[1184,1792]{1,0:T(8,128)}, u32[]{:S(2)}, u32[]{:S(2)}) %collective-permute-start.2) | collective-permute-done | bytes 8486944 | tf_op jit(solution)/shard_map/ppermute | solution.py:9
  788.3 14.1 %subtract_bitcast_fusion = f32[1,1184,1792]{2,1,0:T(8,128)} fusion(f32[1184,1792]{1,0:T(8,128)} %fusion.1, f32[1184,1792]{1,0:T(8,128)} %collective-permute-done.3, f32[1184,1792]{1,0:T(8,128)} %collective-permute-done.2, f32[1184,1792]{1,0:T(8,128)S(1)} %bitcast.29, f32[]{:T(128)} %get-tuple-element.7, f32[]{:T(128)} %get-tuple-element.6, f32[]{:T(128)S(6)} %sub.29), kind=kLoop, calls=%fused_computation.7 | loop fusion | flops 12730368 | bytes 42434572 | tf_op jit(solution)/shard_map/broadcast_in_dim | solution.py:59
  (41 shorter events, 2.7 us)
Async XLA Ops:
  6.5 3.3 copy-start
  6.5 58.2 %all-gather.3.cloned.1.call-start = ((), (), s32[]{:S(2)}) async-start(), calls=%async_computation | async-start | bytes 4128768 | tf_op jit(solution)/shard_map/all_gather | solution.py:31
  27.5 73.6 %all-gather.5.cloned.1.call-start = ((), (), s32[]{:S(2)}) async-start(), calls=%async_computation.2 | async-start | bytes 4128768 | tf_op jit(solution)/shard_map/all_gather | solution.py:34
  28.5 370.1 %all-reduce.3.cloned.1.call-start = ((), (), s32[]{:S(2)}) async-start(), calls=%async_computation.1 | async-start | bytes 14680064 | tf_op jit(solution)/shard_map/psum | solution.py:41
  28.6 188.4 %collective-permute-start = (f32[1184,1792]{1,0:T(8,128)}, f32[1184,1792]{1,0:T(8,128)}, u32[]{:S(2)}, u32[]{:S(2)}) collective-permute-start(f32[1184,1792]{1,0:T(8,128)} %bitcast.30), channel_id=1, source_target_pairs={{0,24},{8,0},{16,8},{24,16},{1,25},{9,1},{17,9},{25,17},{2,26},{10... | collective-permute-start | bytes 25460744 | tf_op jit(solution)/shard_map/ppermute | solution.py:9
  33.7 364.9 %collective-permute-start.1 = (f32[1184,1792]{1,0:T(8,128)}, f32[1184,1792]{1,0:T(8,128)}, u32[]{:S(2)}, u32[]{:S(2)}) collective-permute-start(f32[1184,1792]{1,0:T(8,128)} %bitcast.31), channel_id=1, source_target_pairs={{0,8},{8,16},{16,24},{24,0},{1,9},{9,17},{17,25},{25,1},{2,10},{10... | collective-permute-start | bytes 25460744 | tf_op jit(solution)/shard_map/ppermute | solution.py:9
  64.8 7.6 copy-start.5
  64.8 17.1 %slice-start.3 = ((s8[8486912]{0:T(1024)(128)(4,1)}), s8[4194304]{0:T(1024)(128)(4,1)S(1)}, s32[]{:S(2)}) async-start(s8[8486912]{0:T(1024)(128)(4,1)} %bitcast.32), calls=%async_computation.7 | async-start | bytes 8388608
  64.8 17.1 %slice-start.4 = ((s8[8486912]{0:T(1024)(128)(4,1)}), s8[4194304]{0:T(1024)(128)(4,1)S(1)}, s32[]{:S(2)}) async-start(s8[8486912]{0:T(1024)(128)(4,1)} %bitcast.32), calls=%async_computation.8 | async-start | bytes 8388608
  72.4 9.5 %slice-start.5 = ((s8[8486912]{0:T(1024)(128)(4,1)}), s8[98304]{0:T(1024)(128)(4,1)S(1)}, s32[]{:S(2)}) async-start(s8[8486912]{0:T(1024)(128)(4,1)} %bitcast.32), calls=%async_computation.9 | async-start | bytes 196608
  80.4 1.5 copy-start.2
  89.1 0.7 copy-start.4
  89.1 458.6 %all-reduce.5.cloned.1.call-start = ((), (), s32[]{:S(2)}) async-start(), calls=%async_computation.3 | async-start | bytes 14680064 | tf_op jit(solution)/shard_map/psum | solution.py:41
  421.2 187.5 %collective-permute-start.3 = (f32[1184,1792]{1,0:T(8,128)}, f32[1184,1792]{1,0:T(8,128)}, u32[]{:S(2)}, u32[]{:S(2)}) collective-permute-start(f32[1184,1792]{1,0:T(8,128)} %get-tuple-element.8), channel_id=1, source_target_pairs={{0,8},{8,16},{16,24},{24,0},{1,9},{9,17},{17,25},{25,1},{2,10},{10... | collective-permute-start | bytes 25460744 | tf_op jit(solution)/shard_map/ppermute | solution.py:9
  422.9 365.4 %collective-permute-start.2 = (f32[1184,1792]{1,0:T(8,128)}, f32[1184,1792]{1,0:T(8,128)}, u32[]{:S(2)}, u32[]{:S(2)}) collective-permute-start(f32[1184,1792]{1,0:T(8,128)} %get-tuple-element.8), channel_id=1, source_target_pairs={{0,24},{8,0},{16,8},{24,16},{1,25},{9,1},{17,9},{25,17},{2,26},{10... | collective-permute-start | bytes 25460744 | tf_op jit(solution)/shard_map/ppermute | solution.py:9
  433.8 113.8 %copy-start.3 = (bf16[1024,1184]{0,1:T(8,128)(2,1)S(1)}, bf16[1024,1184]{0,1:T(8,128)(2,1)}, u32[]{:S(2)}) copy-start(bf16[1024,1184]{0,1:T(8,128)(2,1)} %copy-done.2) | copy-start | bytes 7274500
  433.8 354.5 %slice-start = ((s8[8486912]{0:T(1024)(128)(4,1)}), s8[98304]{0:T(1024)(128)(4,1)S(1)}, s32[]{:S(2)}) async-start(s8[8486912]{0:T(1024)(128)(4,1)} %bitcast.28), calls=%async_computation.4 | async-start | bytes 196608
  547.6 240.6 %slice-start.1 = ((s8[8486912]{0:T(1024)(128)(4,1)}), s8[4194304]{0:T(1024)(128)(4,1)S(1)}, s32[]{:S(2)}) async-start(s8[8486912]{0:T(1024)(128)(4,1)} %bitcast.28), calls=%async_computation.5 | async-start | bytes 8388608
  547.6 240.6 %slice-start.2 = ((s8[8486912]{0:T(1024)(128)(4,1)}), s8[4194304]{0:T(1024)(128)(4,1)S(1)}, s32[]{:S(2)}) async-start(s8[8486912]{0:T(1024)(128)(4,1)} %bitcast.28), calls=%async_computation.6 | async-start | bytes 8388608
  788.3 14.2 %copy-start.1 = (s32[4,1024]{1,0:T(4,128)S(1)}, s32[4,1024]{1,0:T(4,128)}, u32[]{:S(2)}) copy-start(s32[4,1024]{1,0:T(4,128)} %param.15) | copy-start | bytes 49156
Sparse Core Ops, SparseCore 0:
  27.6 37.0 all-gather.2
  66.7 34.3 all-gather.4
  104.4 115.4 all-reduce.2
  433.9 113.6 all-reduce.4
where the time goes:
time: 809 us
  waiting for transfers between devices  680 us (84%)
  matrix products  66.9 us (8%)
  local copies, waits for them, and re-layouts  20.5 us (3%)
  between operations  16.4 us (2%)
  other arithmetic  16.3 us (2%)
  starting transfers between devices  9.08 us (1%)
    ppermute x4, waiting for transfers between devices, shifted(): lax.ppermute(array, axis, [(i, (i + by) % count) for i in range(count)])  525 us
    psum x2, waiting for transfers between devices, gradient(): output = lax.psum(partial_out, 'tp')  114 us
    dot_general x2, matrix products, gradient(): lax.dot_general(hidden, resid, (((0,), (0,)), ((), ())), preferred_elemen...  35.4 us
    all_gather x1, waiting for transfers between devices, body(): rows = lax.all_gather(inputs_local, 'tp', axis=1, tiled=True)  31 us
  transfers between devices with their start and end apart: 8, of which 7 were waited for; matrix products, arithmetic and copies ran while one was open for 6% of the time, Pallas kernels for 0%

commit v1 on v0

--- a/solution.py
+++ b/solution.py
@@ -38,7 +38,9 @@
     def gradient(weights):
         weights_half = weights.astype(jnp.bfloat16)
         partial_out = scale * jnp.dot(hidden, weights_half, preferred_element_type=jnp.float32)
-        output = lax.psum(partial_out, "tp")
+        output = partial_out
+        for hop in (1, 2, 4):
+            output = output + lax.ppermute(output, "tp", [(dev, dev ^ hop) for dev in range(8)])
         resid = (output - teacher_full.astype(jnp.float32)).astype(jnp.bfloat16)
         return scale * lax.dot_general(
             hidden, resid, (((0,), (0,)), ((), ())), preferred_element_type=jnp.float32

time: 809 us -> 930 us (1.15)
  waiting for transfers between devices: 680 us -> 756 us
  local copies, waits for them, and re-layouts: 20.5 us -> 36.9 us
  matrix products: 66.9 us -> 79.6 us
  other arithmetic: 16.3 us -> 28.3 us
    ppermute x0 -> x6, waiting for transfers between devices: none -> 328 us  [gradient(): lax.ppermute(output, 'tp', [(dev, dev ^ hop) for dev in range(8)])]
    ppermute x4, waiting for transfers between devices: 525 us -> 343 us  [shifted(): lax.ppermute(array, axis, [(i, (i + by) % count) for i in range(count)])]
    psum x2 -> x0, waiting for transfers between devices: 114 us -> none  [gradient(): output = lax.psum(partial_out, 'tp')]
    all_gather x1, waiting for transfers between devices: 9.5 us -> 47.7 us  [body(): teacher = lax.all_gather(teacher_local, 'tp', axis=1, tiled=True)]
    add x0 -> x4, other arithmetic: none -> 25 us  [gradient(): output + lax.ppermute(output, 'tp', [(dev, dev ^ hop) for dev in range(8)])]
    dot_general x2, matrix products: 35.4 us -> 50.6 us  [gradient(): lax.dot_general(hidden, resid, (((0,), (0,)), ((), ())), preferred_elemen...]
    broadcast_in_dim x1 -> x0, other arithmetic: 14.1 us -> none  [body(): return result[None]]
    unnamed x26, local copies, waits for them, and re-layouts: 9.26 us -> 18.7 us
  transfers between devices with their start and end apart: 8 -> 12, of which waited for: 7 -> 9; matrix products, arithmetic and copies ran while one was open for 6% -> 2% of each run, Pallas kernels for 0% -> 0%
where the time goes in v1:
time: 930 us
  waiting for transfers between devices  756 us (81%)
  matrix products  79.6 us (9%)
  local copies, waits for them, and re-layouts  36.9 us (4%)
  other arithmetic  28.3 us (3%)
  between operations  16.8 us (2%)
  starting transfers between devices  12.1 us (1%)
    ppermute x4, waiting for transfers between devices, shifted(): lax.ppermute(array, axis, [(i, (i + by) % count) for i in range(count)])  343 us
    ppermute x6, waiting for transfers between devices, gradient(): lax.ppermute(output, 'tp', [(dev, dev ^ hop) for dev in range(8)])  328 us
    dot_general x2, matrix products, gradient(): lax.dot_general(hidden, resid, (((0,), (0,)), ((), ())), preferred_elemen...  50.6 us
    all_gather x1, waiting for transfers between devices, body(): teacher = lax.all_gather(teacher_local, 'tp', axis=1, tiled=True)  47.7 us
    all_gather x1, waiting for transfers between devices, body(): rows = lax.all_gather(inputs_local, 'tp', axis=1, tiled=True)  37.2 us
    add x4, other arithmetic, gradient(): output + lax.ppermute(output, 'tp', [(dev, dev ^ hop) for dev in range(8)])  25 us
    unnamed x26, local copies, waits for them, and re-layouts  18.7 us
  transfers between devices with their start and end apart: 12, of which 9 were waited for; matrix products, arithmetic and copies ran while one was open for 2% of the time, Pallas kernels for 0%

profile of v1, /device:TPU:0, one launch (start us, length us, event | category | flops | bytes accessed | tf_op | source)
XLA Modules:
  0.0 929.8 jit_solution(13921809371300892428)
XLA Ops:
  9.8 4.0 copy.13
  13.8 3.2 copy.11
  17.0 5.3 gather_fusion.1
  22.4 5.0 gather_fusion
  29.6 37.2 %all-gather.3.cloned.1.call-done = bf16[1024,1792]{0,1:T(8,128)(2,1)} async-done(((bf16[1024,224]{0,1:T(8,128)(2,1)}), bf16[1024,1792]{0,1:T(8,128)(2,1)}) %all-gather.3.cloned.1.call-update) | async-done | bytes 3670032 | tf_op jit(solution)/shard_map/all_gather | solution.py:31
  66.9 7.6 fusion.17
  74.4 7.7 multiply_convert_fusion
  82.2 5.2 convolution_multiply_fusion.2
  90.5 8.8 collective-permute-done.2
  99.3 6.1 add.56
  110.7 154.9 %collective-permute-done.3 = f32[1024,1792]{1,0:T(8,128)} collective-permute-done((f32[1024,1792]{1,0:T(8,128)S(1)}, f32[1024,1792]{1,0:T(8,128)}, u32[]{:S(2)}, u32[]{:S(2)}) %collective-permute-start.3) | collective-permute-done | bytes 7340064 | tf_op jit(solution)/shard_map/ppermute | solution.py:43
  265.7 6.8 add.57
  276.8 47.7 %all-gather.5.cloned.1.call-done = bf16[1024,1792]{0,1:T(8,128)(2,1)} async-done(((bf16[1024,224]{0,1:T(8,128)(2,1)}), bf16[1024,1792]{0,1:T(8,128)(2,1)}) %all-gather.5.cloned.1.call-update) | async-done | bytes 3670032 | tf_op jit(solution)/shard_map/all_gather | solution.py:34
  324.5 6.0 copy.15
  330.5 144.3 %collective-permute-done = f32[1184,1792]{1,0:T(8,128)} collective-permute-done((f32[1184,1792]{1,0:T(8,128)}, f32[1184,1792]{1,0:T(8,128)}, u32[]{:S(2)}, u32[]{:S(2)}) %collective-permute-start) | collective-permute-done | bytes 8486944 | tf_op jit(solution)/shard_map/ppermute | solution.py:9
  474.7 26.8 %multiply_subtract_fusion = (f32[1184,1792]{1,0:T(8,128)}, f32[1184,1792]{1,0:T(8,128)}, f32[1184,1792]{1,0:T(8,128)}) fusion(f32[1184,1792]{1,0:T(8,128)} %collective-permute-done.1, f32[]{:T(128)} %get-tuple-element.7, f32[1184,1792]{1,0:T(8,128)} %collective-permute-done, f32[]{:T(128)} %get-tuple-element.6, f32[1,1184,1792]{2,1,0:T(8,128)} %param.14, ...), kind=kOutput, calls=%fused_computation.9 | convolution fusion | flops 4369612800 | bytes 71696400 | tf_op jit(solution)/shard_map/dot_general | solution.py:45
  501.6 8.6 convolution_multiply_fusion.1
  513.1 9.0 collective-permute-done.7
  522.0 6.1 add.61
  532.6 155.7 %collective-permute-done.8 = f32[1024,1792]{1,0:T(8,128)} collective-permute-done((f32[1024,1792]{1,0:T(8,128)S(1)}, f32[1024,1792]{1,0:T(8,128)}, u32[]{:S(2)}, u32[]{:S(2)}) %collective-permute-start.8) | collective-permute-done | bytes 7340064 | tf_op jit(solution)/shard_map/ppermute | solution.py:43
  688.3 6.1 add.62
  697.8 18.5 %collective-permute-done.6 = f32[1184,1792]{1,0:T(8,128)} collective-permute-done((f32[1184,1792]{1,0:T(8,128)}, f32[1184,1792]{1,0:T(8,128)}, u32[]{:S(2)}, u32[]{:S(2)}) %collective-permute-start.6) | collective-permute-done | bytes 8486944 | tf_op jit(solution)/shard_map/ppermute | solution.py:9
  716.3 179.8 %collective-permute-done.5 = f32[1184,1792]{1,0:T(8,128)} collective-permute-done((f32[1184,1792]{1,0:T(8,128)}, f32[1184,1792]{1,0:T(8,128)}, u32[]{:S(2)}, u32[]{:S(2)}) %collective-permute-start.5) | collective-permute-done | bytes 8486944 | tf_op jit(solution)/shard_map/ppermute | solution.py:9
  899.2 23.7 %subtract_bitcast_fusion = f32[1,1184,1792]{2,1,0:T(8,128)} fusion(f32[1184,1792]{1,0:T(8,128)} %collective-permute-done.6, f32[1184,1792]{1,0:T(8,128)} %collective-permute-done.5, f32[1184,1792]{1,0:T(8,128)} %get-tuple-element.12, bf16[1024,1184]{0,1:T(8,128)(2,1)S(1)} %multiply_convert_fusion, f32[]{:T(128)} %get-tuple-element.7, f32[]{:T(128)} %get-tuple-element.6, ...), kind=kOutput, calls=%fused_computation.7 | convolution fusion | flops 4378099712 | bytes 63209484 | tf_op jit(solution)/shard_map/dot_general | solution.py:45
  (50 shorter events, 28.8 us)
Async XLA Ops:
  6.5 3.3 copy-start
  6.5 60.3 %all-gather.3.cloned.1.call-start = ((), (), s32[]{:S(2)}) async-start(), calls=%async_computation | async-start | bytes 4128768 | tf_op jit(solution)/shard_map/all_gather | solution.py:31
  29.6 294.9 %all-gather.5.cloned.1.call-start = ((), (), s32[]{:S(2)}) async-start(), calls=%async_computation.1 | async-start | bytes 4128768 | tf_op jit(solution)/shard_map/all_gather | solution.py:34
  66.8 7.6 copy-start.8
  66.9 15.3 %slice-start = ((s8[8486912]{0:T(1024)(128)(4,1)}), s8[4194304]{0:T(1024)(128)(4,1)S(1)}, s32[]{:S(2)}) async-start(s8[8486912]{0:T(1024)(128)(4,1)} %bitcast.29), calls=%async_computation.2 | async-start | bytes 8388608
  66.9 15.4 %slice-start.1 = ((s8[8486912]{0:T(1024)(128)(4,1)}), s8[4194304]{0:T(1024)(128)(4,1)S(1)}, s32[]{:S(2)}) async-start(s8[8486912]{0:T(1024)(128)(4,1)} %bitcast.29), calls=%async_computation.3 | async-start | bytes 8388608
  74.4 7.8 slice-start.2
  87.4 3.1 copy-start.5
  87.4 11.9 %collective-permute-start.2 = (f32[1024,1792]{1,0:T(8,128)S(1)}, f32[1024,1792]{1,0:T(8,128)}, u32[]{:S(2)}, u32[]{:S(2)}) collective-permute-start(f32[1024,1792]{1,0:T(8,128)S(1)} %convolution_multiply_fusion.2), channel_id=1, source_target_pairs={{0,1},{1,0},{2,3},{3,2},{4,5},{5,4},{6,7},{7,6},{8,9},{9,8},{10,11... | collective-permute-start | bytes 22020104 | tf_op jit(solution)/shard_map/ppermute | solution.py:43
  105.4 160.3 %collective-permute-start.3 = (f32[1024,1792]{1,0:T(8,128)S(1)}, f32[1024,1792]{1,0:T(8,128)}, u32[]{:S(2)}, u32[]{:S(2)}) collective-permute-start(f32[1024,1792]{1,0:T(8,128)S(1)} %add.56), channel_id=1, source_target_pairs={{0,2},{1,3},{2,0},{3,1},{4,6},{5,7},{6,4},{7,5},{8,10},{9,11},{10,... | collective-permute-start | bytes 22020104 | tf_op jit(solution)/shard_map/ppermute | solution.py:43
  106.9 167.9 %copy-start.7 = (f32[4]{0:T(128)S(1)}, f32[4]{0:T(128)}, u32[]{:S(2)}) copy-start(f32[4]{0:T(128)} %param.17) | copy-start | bytes 52
  106.9 223.6 %collective-permute-start.1 = (f32[1184,1792]{1,0:T(8,128)}, f32[1184,1792]{1,0:T(8,128)}, u32[]{:S(2)}, u32[]{:S(2)}) collective-permute-start(f32[1184,1792]{1,0:T(8,128)} %bitcast.27), channel_id=1, source_target_pairs={{0,8},{8,16},{16,24},{24,0},{1,9},{9,17},{17,25},{25,1},{2,10},{10... | collective-permute-start | bytes 25460744 | tf_op jit(solution)/shard_map/ppermute | solution.py:9
  108.4 366.3 %collective-permute-start = (f32[1184,1792]{1,0:T(8,128)}, f32[1184,1792]{1,0:T(8,128)}, u32[]{:S(2)}, u32[]{:S(2)}) collective-permute-start(f32[1184,1792]{1,0:T(8,128)} %bitcast.28), channel_id=1, source_target_pairs={{0,24},{8,0},{16,8},{24,16},{1,25},{9,1},{17,9},{25,17},{2,26},{10... | collective-permute-start | bytes 25460744 | tf_op jit(solution)/shard_map/ppermute | solution.py:9
  272.5 202.2 %collective-permute-start.4 = (f32[1024,1792]{1,0:T(8,128)}, f32[1024,1792]{1,0:T(8,128)}, u32[]{:S(2)}, u32[]{:S(2)}) collective-permute-start(f32[1024,1792]{1,0:T(8,128)} %add.57), channel_id=1, source_target_pairs={{0,4},{1,5},{2,6},{3,7},{4,0},{5,1},{6,2},{7,3},{8,12},{9,13},{10,... | collective-permute-start | bytes 22020104 | tf_op jit(solution)/shard_map/ppermute | solution.py:43
  510.2 2.9 copy-start.6
  510.2 11.9 %collective-permute-start.7 = (f32[1024,1792]{1,0:T(8,128)S(1)}, f32[1024,1792]{1,0:T(8,128)}, u32[]{:S(2)}, u32[]{:S(2)}) collective-permute-start(f32[1024,1792]{1,0:T(8,128)S(1)} %convolution_multiply_fusion.1), channel_id=1, source_target_pairs={{0,1},{1,0},{2,3},{3,2},{4,5},{5,4},{6,7},{7,6},{8,9},{9,8},{10,11... | collective-permute-start | bytes 22020104 | tf_op jit(solution)/shard_map/ppermute | solution.py:43
  528.1 4.5 copy-start.3
  528.1 160.2 %collective-permute-start.8 = (f32[1024,1792]{1,0:T(8,128)S(1)}, f32[1024,1792]{1,0:T(8,128)}, u32[]{:S(2)}, u32[]{:S(2)}) collective-permute-start(f32[1024,1792]{1,0:T(8,128)S(1)} %add.61), channel_id=1, source_target_pairs={{0,2},{1,3},{2,0},{3,1},{4,6},{5,7},{6,4},{7,5},{8,10},{9,11},{10,... | collective-permute-start | bytes 22020104 | tf_op jit(solution)/shard_map/ppermute | solution.py:43
  528.8 187.6 %collective-permute-start.6 = (f32[1184,1792]{1,0:T(8,128)}, f32[1184,1792]{1,0:T(8,128)}, u32[]{:S(2)}, u32[]{:S(2)}) collective-permute-start(f32[1184,1792]{1,0:T(8,128)} %get-tuple-element.8), channel_id=1, source_target_pairs={{0,8},{8,16},{16,24},{24,0},{1,9},{9,17},{17,25},{25,1},{2,10},{10... | collective-permute-start | bytes 25460744 | tf_op jit(solution)/shard_map/ppermute | solution.py:9
  529.9 366.2 %collective-permute-start.5 = (f32[1184,1792]{1,0:T(8,128)}, f32[1184,1792]{1,0:T(8,128)}, u32[]{:S(2)}, u32[]{:S(2)}) collective-permute-start(f32[1184,1792]{1,0:T(8,128)} %get-tuple-element.8), channel_id=1, source_target_pairs={{0,24},{8,0},{16,8},{24,16},{1,25},{9,1},{17,9},{25,17},{2,26},{10... | collective-permute-start | bytes 25460744 | tf_op jit(solution)/shard_map/ppermute | solution.py:9
  694.4 2.9 copy-start.2
  697.2 198.9 %collective-permute-start.9 = (f32[1024,1792]{1,0:T(8,128)S(1)}, f32[1024,1792]{1,0:T(8,128)S(1)}, u32[]{:S(2)}, u32[]{:S(2)}) collective-permute-start(f32[1024,1792]{1,0:T(8,128)S(1)} %add.62), channel_id=1, source_target_pairs={{0,4},{1,5},{2,6},{3,7},{4,0},{5,1},{6,2},{7,3},{8,12},{9,13},{10,... | collective-permute-start | bytes 22020104 | tf_op jit(solution)/shard_map/ppermute | solution.py:43
  896.1 3.0 copy-start.4
  899.2 23.7 %copy-start.1 = (s32[4,1024]{1,0:T(4,128)S(1)}, s32[4,1024]{1,0:T(4,128)}, u32[]{:S(2)}) copy-start(s32[4,1024]{1,0:T(4,128)} %param.15) | copy-start | bytes 49156
Sparse Core Ops, SparseCore 0:
  29.7 37.0 all-gather.2
  274.9 49.4 all-gather.4
